TPU v7x, 32 devices: a whole 2x2x4 slice. The times are simulated.
32 devices in a mesh: group: 4 (over y, core), sub: 8 (over z, x).
Axes of the slice: x: 2, y: 2, z: 4, core: 2. Of those that a mesh axis runs over, the one named last changes fastest.
Arguments:
- shared_sizes: int32 [4, 8, 2], P('group', 'sub'), may hold values from 0 to 256, as said below
- stiffness: float32 [4, 8], P('group', 'sub'), may hold values from 0.1 to 10
- load_cases: float32 [4, 8, 1024, 384], P('group', 'sub'), may hold values from -6 to 6
- schur_blocks: bfloat16 [4, 8, 1024, 1024], P('group', 'sub')
- neumann_inverse: bfloat16 [4, 8, 1024, 1024], P('group', 'sub')
- coarse_basis: bfloat16 [4, 8, 32, 1024], P('group', 'sub'), may hold values from -0.1875 to 0.1875
- coarse_dofs: int32 [4, 8, 32], P('group', 'sub'), may hold values from 0 to 511
- coarse_inverse: float32 [512, 512], P('sub'), as said below
Outputs:
- solution: float32 [4, 8, 1024, 384], P('group', 'sub')
- residual: float32 [4, 8, 1024, 384], P('group', 'sub')
Inputs may be any that keep to these rules, and one draw needn't show every extreme that they name: shared_sizes[g, s, 0] equals shared_sizes[g, s - 1, 1]; the lower share of the first and the upper share of the last subdomain of a group are 0, the other shares lie in 128 to 256, and in every group some subdomain shares exactly 256 with its upper neighbour. `coarse_inverse`: symmetric.
All inputs are finite; a program needn't handle non-finite values.
Results may differ from a plain program's by a relative error of at most 0.0075.
Values sent between devices are 32-bit elements; how exact they have to be, the bound alone decides.
No kernel may reach another device: no remote copies, remote signals or barrier semaphores. Data moves between devices by JAX's collectives and lax.ppermute only.
A program may use at most 128 MiB of HBM per device.

v0:
```python
import jax
import jax.numpy as jnp
from jax import lax
from jax.sharding import PartitionSpec as P

MAXSH = 256
ITERS = 4
OMEGA = 0.6


def from_behind(block, axis, distance):
    devices = range(lax.axis_size(axis))
    route = [(i - distance, i) for i in devices if i - distance in devices]
    return lax.ppermute(block, axis, route)


def extended(x, sides, width):
    for axis, dim in sides:
        peers, length = (lax.axis_size(axis), x.shape[dim])
        up = [(i, (i + 1) % peers) for i in range(peers - 1)]
        down = [(j, i) for i, j in up]
        last = lax.slice_in_dim(x, length - width, length, axis=dim)
        leading = lax.slice_in_dim(x, 0, width, axis=dim)
        before = lax.ppermute(last, axis, up)
        after = lax.ppermute(leading, axis, down)
        x = jnp.concatenate([before, x, after], axis=dim)
    return x


def lift_piece(tail_rows, share_size):
    slab_width = tail_rows.shape[0]
    rolled = jnp.roll(tail_rows, share_size - slab_width, axis=0)
    inside = (jnp.arange(slab_width) < share_size)[:, None]
    return jnp.where(inside, rolled, jnp.zeros_like(rolled))


def place_piece(head_rows, share_size):
    slab_width = head_rows.shape[0]
    inside = (jnp.arange(slab_width) < share_size)[:, None]
    masked = jnp.where(inside, head_rows, jnp.zeros_like(head_rows))
    return jnp.roll(masked, slab_width - share_size, axis=0)


def assemble(vector, share_up):
    unknowns = vector.shape[0]
    tail_rows = vector[unknowns - MAXSH :]
    head_rows = vector[:MAXSH]
    lifted = lift_piece(tail_rows, share_up)
    from_lower = from_behind(lifted, "sub", 1)
    from_upper = from_behind(head_rows, "sub", -1)
    placed = place_piece(from_upper, share_up)
    return jnp.concatenate(
        [head_rows + from_lower, vector[MAXSH : unknowns - MAXSH], tail_rows + placed], axis=0
    )


def on_device(
    shared_sizes,
    stiffness,
    load_cases,
    schur_blocks,
    neumann_inverse,
    coarse_basis,
    coarse_dofs,
    coarse_inverse,
):
    share_low = shared_sizes[0, 0, 0]
    share_up = shared_sizes[0, 0, 1]
    beside_all = extended(stiffness, (("sub", 1),), 1)
    own_stiff = beside_all[0, 1]
    low_weight = own_stiff / (own_stiff + beside_all[0, 0])
    up_weight = own_stiff / (own_stiff + beside_all[0, 2])
    loads = load_cases[0, 0]
    schur = schur_blocks[0, 0]
    neumann = neumann_inverse[0, 0]
    basis = coarse_basis[0, 0]
    my_dofs = coarse_dofs[0, 0]
    unknowns, cases = loads.shape
    own_count = coarse_inverse.shape[0]
    row_index = jnp.arange(unknowns)
    weight = jnp.where(
        row_index < share_low,
        low_weight,
        jnp.where(row_index >= unknowns - share_up, up_weight, jnp.float32(1.0)),
    )[:, None]
    highest = lax.Precision.HIGHEST

    def operator_residual(solution):
        return loads - jnp.dot(
            schur, solution.astype(jnp.bfloat16), preferred_element_type=jnp.float32
        )

    solution = jnp.zeros((unknowns, cases), jnp.float32)
    for sweep in range(ITERS):
        local = operator_residual(solution)
        weighted = (weight * assemble(local, share_up)).astype(jnp.bfloat16)
        coarse_terms = jnp.dot(basis, weighted, preferred_element_type=jnp.float32)
        dof_values = my_dofs.astype(jnp.float32)
        all_terms = lax.all_gather(coarse_terms, "sub", axis=0, tiled=True)
        all_dofs = lax.all_gather(dof_values, "sub", axis=0, tiled=True)
        dof_index = all_dofs.astype(jnp.int32)
        first_row = lax.axis_index("sub") * own_count
        own_select = (dof_index[:, None] == first_row + jnp.arange(own_count)[None, :]).astype(
            jnp.float32
        )
        owned = lax.dot_general(own_select, all_terms, (((0,), (0,)), ((), ())), precision=highest)
        owned = lax.psum(owned, "group")
        columns = jnp.take(coarse_inverse, dof_index, axis=1)
        partial_vals = lax.dot_general(columns, owned, (((0,), (0,)), ((), ())), precision=highest)
        partial_vals = partial_vals.reshape(-1, coarse_terms.shape[0], cases)
        received = lax.all_to_all(partial_vals, "sub", split_axis=0, concat_axis=0, tiled=True)
        picked = jnp.sum(received, axis=0)
        picked = picked.astype(jnp.bfloat16)
        correction = jnp.dot(neumann, weighted, preferred_element_type=jnp.float32)
        correction = correction + lax.dot_general(
            basis, picked, (((0,), (0,)), ((), ())), preferred_element_type=jnp.float32
        )
        solution = solution + OMEGA * assemble(weight * correction, share_up)
    residual = assemble(operator_residual(solution), share_up)
    return (solution[None, None], residual[None, None])


def solution(mesh):
    return jax.shard_map(
        on_device,
        mesh=mesh,
        in_specs=(
            P("group", "sub", None),
            P("group", "sub"),
            P("group", "sub", None, None),
            P("group", "sub", None, None),
            P("group", "sub", None, None),
            P("group", "sub", None, None),
            P("group", "sub", None),
            P("sub", None),
        ),
        out_specs=(P("group", "sub", None, None), P("group", "sub", None, None)),
        check_vma=False,
    )
```

profile of v0, /device:TPU:16, one launch (start us, length us, event | category | flops | bytes accessed | tf_op | source)
XLA Modules:
  0.0 597.5 jit_solution(9661922671992732006)
XLA Ops:
  31.0 14.9 %all-reduce = f32[256]{0:T(256)S(1)} all-reduce(f32[256]{0:T(256)S(1)} %bitcast_dynamic-update-slice_fusion), channel_id=2, replica_groups=mesh['group'=4,'sub'=8] {'sub'}, use_global_device_ids=true, to_apply=%add | all-reduce | flops 256 | bytes 2048
  63.2 27.9 %all_gather.19 = f32[256,384]{1,0:T(8,128)S(1)} all-gather(f32[32,384]{1,0:T(8,128)S(1)} %convolution_bitcast_fusion.3), channel_id=1, replica_groups=mesh['group'=4,'sub'=8] {'sub'}, dimensions={0}, use_global_device_ids=true | all-gather | bytes 442368 | tf_op jit(solution)/shard_map/all_gather | solution.py:99
  93.1 34.8 %all-reduce.6.cloned.1.call-done = f32[64,384]{1,0:T(8,128)} async-done(((f32[64,384]{1,0:T(8,128)}), f32[64,384]{1,0:T(8,128)}) %all-reduce.6.cloned.1.call-update) | async-done | bytes 98320 | tf_op jit(solution)/shard_map/psum | solution.py:107
  129.4 15.0 %all_to_all.20 = f32[8,32,384]{2,1,0:T(8,128)} all-to-all(f32[8,32,384]{2,1,0:T(8,128)S(1)} %bitcast.145), channel_id=1, replica_groups=mesh['group'=4,'sub'=8] {'sub'}, dimensions={0} | all-to-all | bytes 786432 | tf_op jit(solution)/shard_map/all_to_all | solution.py:111
  152.3 8.6 %collective-permute-done.5 = f32[256,384]{0,1:T(8,128)S(1)} collective-permute-done((f32[256,384]{0,1:T(8,128)S(1)}, f32[256,384]{0,1:T(8,128)S(1)}, u32[]{:S(2)}, u32[]{:S(2)}) %collective-permute-start.5) | collective-permute-done | bytes 393248 | tf_op jit(solution)/shard_map/ppermute | solution.py:14
  176.5 8.2 %collective-permute-done.7 = f32[256,384]{0,1:T(8,128)S(1)} collective-permute-done((f32[256,384]{0,1:T(8,128)S(1)}, f32[256,384]{0,1:T(8,128)S(1)}, u32[]{:S(2)}, u32[]{:S(2)}) %collective-permute-start.7) | collective-permute-done | bytes 393248 | tf_op jit(solution)/shard_map/ppermute | solution.py:14
  187.6 8.1 %collective-permute-done.6 = f32[256,384]{0,1:T(8,128)S(1)} collective-permute-done((f32[256,384]{0,1:T(8,128)S(1)}, f32[256,384]{0,1:T(8,128)S(1)}, u32[]{:S(2)}, u32[]{:S(2)}) %collective-permute-start.6) | collective-permute-done | bytes 393248 | tf_op jit(solution)/shard_map/ppermute | solution.py:14
  196.3 25.4 %all_gather.20 = f32[256,384]{1,0:T(8,128)S(1)} all-gather(f32[32,384]{1,0:T(8,128)S(1)} %convolution_bitcast_fusion.2), channel_id=1, replica_groups=mesh['group'=4,'sub'=8] {'sub'}, dimensions={0}, use_global_device_ids=true | all-gather | bytes 442368 | tf_op jit(solution)/shard_map/all_gather | solution.py:99
  222.8 34.4 %all-reduce.8.cloned.1.call-done = f32[64,384]{1,0:T(8,128)} async-done(((f32[64,384]{1,0:T(8,128)}), f32[64,384]{1,0:T(8,128)}) %all-reduce.8.cloned.1.call-update) | async-done | bytes 98320 | tf_op jit(solution)/shard_map/psum | solution.py:107
  258.6 14.9 %all_to_all.21 = f32[8,32,384]{2,1,0:T(8,128)} all-to-all(f32[8,32,384]{2,1,0:T(8,128)S(1)} %bitcast.146), channel_id=1, replica_groups=mesh['group'=4,'sub'=8] {'sub'}, dimensions={0} | all-to-all | bytes 786432 | tf_op jit(solution)/shard_map/all_to_all | solution.py:111
  281.7 8.6 %collective-permute-done.9 = f32[256,384]{0,1:T(8,128)S(1)} collective-permute-done((f32[256,384]{0,1:T(8,128)S(1)}, f32[256,384]{0,1:T(8,128)S(1)}, u32[]{:S(2)}, u32[]{:S(2)}) %collective-permute-start.9) | collective-permute-done | bytes 393248 | tf_op jit(solution)/shard_map/ppermute | solution.py:14
  305.9 8.2 %collective-permute-done.11 = f32[256,384]{0,1:T(8,128)S(1)} collective-permute-done((f32[256,384]{0,1:T(8,128)S(1)}, f32[256,384]{0,1:T(8,128)S(1)}, u32[]{:S(2)}, u32[]{:S(2)}) %collective-permute-start.11) | collective-permute-done | bytes 393248 | tf_op jit(solution)/shard_map/ppermute | solution.py:14
  325.7 25.4 %all_gather.21 = f32[256,384]{1,0:T(8,128)S(1)} all-gather(f32[32,384]{1,0:T(8,128)S(1)} %convolution_bitcast_fusion.1), channel_id=1, replica_groups=mesh['group'=4,'sub'=8] {'sub'}, dimensions={0}, use_global_device_ids=true | all-gather | bytes 442368 | tf_op jit(solution)/shard_map/all_gather | solution.py:99
  352.2 34.4 %all-reduce.10.cloned.1.call-done = f32[64,384]{1,0:T(8,128)} async-done(((f32[64,384]{1,0:T(8,128)}), f32[64,384]{1,0:T(8,128)}) %all-reduce.10.cloned.1.call-update) | async-done | bytes 98320 | tf_op jit(solution)/shard_map/psum | solution.py:107
  388.0 14.9 %all_to_all.22 = f32[8,32,384]{2,1,0:T(8,128)} all-to-all(f32[8,32,384]{2,1,0:T(8,128)S(1)} %bitcast.147), channel_id=1, replica_groups=mesh['group'=4,'sub'=8] {'sub'}, dimensions={0} | all-to-all | bytes 786432 | tf_op jit(solution)/shard_map/all_to_all | solution.py:111
  411.1 8.6 %collective-permute-done.13 = f32[256,384]{0,1:T(8,128)S(1)} collective-permute-done((f32[256,384]{0,1:T(8,128)S(1)}, f32[256,384]{0,1:T(8,128)S(1)}, u32[]{:S(2)}, u32[]{:S(2)}) %collective-permute-start.13) | collective-permute-done | bytes 393248 | tf_op jit(solution)/shard_map/ppermute | solution.py:14
  435.4 8.2 %collective-permute-done.15 = f32[256,384]{0,1:T(8,128)S(1)} collective-permute-done((f32[256,384]{0,1:T(8,128)S(1)}, f32[256,384]{0,1:T(8,128)S(1)}, u32[]{:S(2)}, u32[]{:S(2)}) %collective-permute-start.15) | collective-permute-done | bytes 393248 | tf_op jit(solution)/shard_map/ppermute | solution.py:14
  446.5 8.1 %collective-permute-done.14 = f32[256,384]{0,1:T(8,128)S(1)} collective-permute-done((f32[256,384]{0,1:T(8,128)S(1)}, f32[256,384]{0,1:T(8,128)S(1)}, u32[]{:S(2)}, u32[]{:S(2)}) %collective-permute-start.14) | collective-permute-done | bytes 393248 | tf_op jit(solution)/shard_map/ppermute | solution.py:14
  455.2 25.4 %all_gather.22 = f32[256,384]{1,0:T(8,128)S(1)} all-gather(f32[32,384]{1,0:T(8,128)S(1)} %convolution_bitcast_fusion), channel_id=1, replica_groups=mesh['group'=4,'sub'=8] {'sub'}, dimensions={0}, use_global_device_ids=true | all-gather | bytes 442368 | tf_op jit(solution)/shard_map/all_gather | solution.py:99
  481.6 34.4 %all-reduce.12.cloned.1.call-done = f32[64,384]{1,0:T(8,128)} async-done(((f32[64,384]{1,0:T(8,128)}), f32[64,384]{1,0:T(8,128)}) %all-reduce.12.cloned.1.call-update) | async-done | bytes 98320 | tf_op jit(solution)/shard_map/psum | solution.py:107
  517.5 14.9 %all_to_all.23 = f32[8,32,384]{2,1,0:T(8,128)} all-to-all(f32[8,32,384]{2,1,0:T(8,128)S(1)} %bitcast.144), channel_id=1, replica_groups=mesh['group'=4,'sub'=8] {'sub'}, dimensions={0} | all-to-all | bytes 786432 | tf_op jit(solution)/shard_map/all_to_all | solution.py:111
  540.6 8.6 %collective-permute-done.17 = f32[256,384]{0,1:T(8,128)S(1)} collective-permute-done((f32[256,384]{0,1:T(8,128)S(1)}, f32[256,384]{0,1:T(8,128)S(1)}, u32[]{:S(2)}, u32[]{:S(2)}) %collective-permute-start.17) | collective-permute-done | bytes 393248 | tf_op jit(solution)/shard_map/ppermute | solution.py:14
  552.6 8.7 %collective-permute-done.16 = f32[256,384]{0,1:T(8,128)S(1)} collective-permute-done((f32[256,384]{0,1:T(8,128)S(1)}, f32[256,384]{0,1:T(8,128)S(1)}, u32[]{:S(2)}, u32[]{:S(2)}) %collective-permute-start.16) | collective-permute-done | bytes 393248 | tf_op jit(solution)/shard_map/ppermute | solution.py:14
  565.0 8.2 %collective-permute-done.19 = f32[256,384]{0,1:T(8,128)S(1)} collective-permute-done((f32[256,384]{0,1:T(8,128)S(1)}, f32[256,384]{0,1:T(8,128)S(1)}, u32[]{:S(2)}, u32[]{:S(2)}) %collective-permute-start.19) | collective-permute-done | bytes 393248 | tf_op jit(solution)/shard_map/ppermute | solution.py:14
  (223 shorter events, 168.8 us)
Async XLA Ops:
  7.2 120.8 %all-reduce.6.cloned.1.call-start = ((), (), s32[]{:S(2)}) async-start(), calls=%async_computation.4 | async-start | bytes 196608 | tf_op jit(solution)/shard_map/psum | solution.py:107
  7.2 45.2 %collective-permute-start.1 = (f32[1,1]{1,0:T(1,128)}, f32[1,1]{1,0:T(1,128)}, u32[]{:S(2)}, u32[]{:S(2)}) collective-permute-start(f32[1,1]{1,0:T(1,128)} %param.13), channel_id=1, source_target_pairs={{1,0},{2,1},{3,2},{4,3},{5,4},{6,5},{7,6},{9,8},{10,9},{11,10},{12... | collective-permute-start | bytes 20 | tf_op jit(solution)/shard_map/ppermute | solution.py:25
  10.7 42.5 %collective-permute-start = (f32[1,1]{1,0:T(1,128)}, f32[1,1]{1,0:T(1,128)}, u32[]{:S(2)}, u32[]{:S(2)}) collective-permute-start(f32[1,1]{1,0:T(1,128)} %param.13), channel_id=1, source_target_pairs={{0,1},{1,2},{2,3},{3,4},{4,5},{5,6},{6,7},{8,9},{9,10},{10,11},{11... | collective-permute-start | bytes 20 | tf_op jit(solution)/shard_map/ppermute | solution.py:24
  20.8 25.8 %collective-permute-start.3 = (f32[256,384]{0,1:T(8,128)}, f32[256,384]{0,1:T(8,128)S(1)}, u32[]{:S(2)}, u32[]{:S(2)}) collective-permute-start(f32[256,384]{0,1:T(8,128)} %get-tuple-element.51), channel_id=1, source_target_pairs={{1,0},{2,1},{3,2},{4,3},{5,4},{6,5},{7,6},{9,8},{10,9},{11,10},{12... | collective-permute-start | bytes 1179656 | tf_op jit(solution)/shard_map/ppermute | solution.py:14
  49.6 11.0 %collective-permute-start.2 = (f32[256,384]{0,1:T(8,128)}, f32[256,384]{0,1:T(8,128)}, u32[]{:S(2)}, u32[]{:S(2)}) collective-permute-start(f32[256,384]{0,1:T(8,128)} %get-tuple-element.70), channel_id=1, source_target_pairs={{0,1},{1,2},{2,3},{3,4},{4,5},{5,6},{6,7},{8,9},{9,10},{10,11},{11... | collective-permute-start | bytes 1179656 | tf_op jit(solution)/shard_map/ppermute | solution.py:14
  92.2 165.0 %all-reduce.8.cloned.1.call-start = ((), (), s32[]{:S(2)}) async-start(), calls=%async_computation.5 | async-start | bytes 196608 | tf_op jit(solution)/shard_map/psum | solution.py:107
  149.1 11.8 %collective-permute-start.5 = (f32[256,384]{0,1:T(8,128)S(1)}, f32[256,384]{0,1:T(8,128)S(1)}, u32[]{:S(2)}, u32[]{:S(2)}) collective-permute-start(f32[256,384]{0,1:T(8,128)S(1)} %get-tuple-element.47), channel_id=1, source_target_pairs={{1,0},{2,1},{3,2},{4,3},{5,4},{6,5},{7,6},{9,8},{10,9},{11,10},{12... | collective-permute-start | bytes 1179656 | tf_op jit(solution)/shard_map/ppermute | solution.py:14
  161.2 11.9 %collective-permute-start.4 = (f32[256,384]{0,1:T(8,128)S(1)}, f32[256,384]{0,1:T(8,128)S(1)}, u32[]{:S(2)}, u32[]{:S(2)}) collective-permute-start(f32[256,384]{0,1:T(8,128)S(1)} %get-tuple-element.66), channel_id=1, source_target_pairs={{0,1},{1,2},{2,3},{3,4},{4,5},{5,6},{6,7},{8,9},{9,10},{10,11},{11... | collective-permute-start | bytes 1179656 | tf_op jit(solution)/shard_map/ppermute | solution.py:14
  174.6 10.1 %collective-permute-start.7 = (f32[256,384]{0,1:T(8,128)S(1)}, f32[256,384]{0,1:T(8,128)S(1)}, u32[]{:S(2)}, u32[]{:S(2)}) collective-permute-start(f32[256,384]{0,1:T(8,128)S(1)} %get-tuple-element.41), channel_id=1, source_target_pairs={{1,0},{2,1},{3,2},{4,3},{5,4},{6,5},{7,6},{9,8},{10,9},{11,10},{12... | collective-permute-start | bytes 1179656 | tf_op jit(solution)/shard_map/ppermute | solution.py:14
  185.0 10.7 %collective-permute-start.6 = (f32[256,384]{0,1:T(8,128)S(1)}, f32[256,384]{0,1:T(8,128)S(1)}, u32[]{:S(2)}, u32[]{:S(2)}) collective-permute-start(f32[256,384]{0,1:T(8,128)S(1)} %get-tuple-element.64), channel_id=1, source_target_pairs={{0,1},{1,2},{2,3},{3,4},{4,5},{5,6},{6,7},{8,9},{9,10},{10,11},{11... | collective-permute-start | bytes 1179656 | tf_op jit(solution)/shard_map/ppermute | solution.py:14
  222.7 163.8 %all-reduce.10.cloned.1.call-start = ((), (), s32[]{:S(2)}) async-start(), calls=%async_computation.6 | async-start | bytes 196608 | tf_op jit(solution)/shard_map/psum | solution.py:107
  278.5 11.8 %collective-permute-start.9 = (f32[256,384]{0,1:T(8,128)S(1)}, f32[256,384]{0,1:T(8,128)S(1)}, u32[]{:S(2)}, u32[]{:S(2)}) collective-permute-start(f32[256,384]{0,1:T(8,128)S(1)} %get-tuple-element.37), channel_id=1, source_target_pairs={{1,0},{2,1},{3,2},{4,3},{5,4},{6,5},{7,6},{9,8},{10,9},{11,10},{12... | collective-permute-start | bytes 1179656 | tf_op jit(solution)/shard_map/ppermute | solution.py:14
  290.6 11.9 %collective-permute-start.8 = (f32[256,384]{0,1:T(8,128)S(1)}, f32[256,384]{0,1:T(8,128)S(1)}, u32[]{:S(2)}, u32[]{:S(2)}) collective-permute-start(f32[256,384]{0,1:T(8,128)S(1)} %get-tuple-element.62), channel_id=1, source_target_pairs={{0,1},{1,2},{2,3},{3,4},{4,5},{5,6},{6,7},{8,9},{9,10},{10,11},{11... | collective-permute-start | bytes 1179656 | tf_op jit(solution)/shard_map/ppermute | solution.py:14
  303.9 10.1 %collective-permute-start.11 = (f32[256,384]{0,1:T(8,128)S(1)}, f32[256,384]{0,1:T(8,128)S(1)}, u32[]{:S(2)}, u32[]{:S(2)}) collective-permute-start(f32[256,384]{0,1:T(8,128)S(1)} %get-tuple-element.31), channel_id=1, source_target_pairs={{1,0},{2,1},{3,2},{4,3},{5,4},{6,5},{7,6},{9,8},{10,9},{11,10},{12... | collective-permute-start | bytes 1179656 | tf_op jit(solution)/shard_map/ppermute | solution.py:14
  314.3 10.7 %collective-permute-start.10 = (f32[256,384]{0,1:T(8,128)S(1)}, f32[256,384]{0,1:T(8,128)S(1)}, u32[]{:S(2)}, u32[]{:S(2)}) collective-permute-start(f32[256,384]{0,1:T(8,128)S(1)} %get-tuple-element.60), channel_id=1, source_target_pairs={{0,1},{1,2},{2,3},{3,4},{4,5},{5,6},{6,7},{8,9},{9,10},{10,11},{11... | collective-permute-start | bytes 1179656 | tf_op jit(solution)/shard_map/ppermute | solution.py:14
  352.1 163.9 %all-reduce.12.cloned.1.call-start = ((), (), s32[]{:S(2)}) async-start(), calls=%async_computation.7 | async-start | bytes 196608 | tf_op jit(solution)/shard_map/psum | solution.py:107
  407.9 11.9 %collective-permute-start.13 = (f32[256,384]{0,1:T(8,128)S(1)}, f32[256,384]{0,1:T(8,128)S(1)}, u32[]{:S(2)}, u32[]{:S(2)}) collective-permute-start(f32[256,384]{0,1:T(8,128)S(1)} %get-tuple-element.27), channel_id=1, source_target_pairs={{1,0},{2,1},{3,2},{4,3},{5,4},{6,5},{7,6},{9,8},{10,9},{11,10},{12... | collective-permute-start | bytes 1179656 | tf_op jit(solution)/shard_map/ppermute | solution.py:14
  420.0 11.9 %collective-permute-start.12 = (f32[256,384]{0,1:T(8,128)S(1)}, f32[256,384]{0,1:T(8,128)S(1)}, u32[]{:S(2)}, u32[]{:S(2)}) collective-permute-start(f32[256,384]{0,1:T(8,128)S(1)} %get-tuple-element.58), channel_id=1, source_target_pairs={{0,1},{1,2},{2,3},{3,4},{4,5},{5,6},{6,7},{8,9},{9,10},{10,11},{11... | collective-permute-start | bytes 1179656 | tf_op jit(solution)/shard_map/ppermute | solution.py:14
  433.4 10.1 %collective-permute-start.15 = (f32[256,384]{0,1:T(8,128)S(1)}, f32[256,384]{0,1:T(8,128)S(1)}, u32[]{:S(2)}, u32[]{:S(2)}) collective-permute-start(f32[256,384]{0,1:T(8,128)S(1)} %get-tuple-element.21), channel_id=1, source_target_pairs={{1,0},{2,1},{3,2},{4,3},{5,4},{6,5},{7,6},{9,8},{10,9},{11,10},{12... | collective-permute-start | bytes 1179656 | tf_op jit(solution)/shard_map/ppermute | solution.py:14
  443.9 10.7 %collective-permute-start.14 = (f32[256,384]{0,1:T(8,128)S(1)}, f32[256,384]{0,1:T(8,128)S(1)}, u32[]{:S(2)}, u32[]{:S(2)}) collective-permute-start(f32[256,384]{0,1:T(8,128)S(1)} %get-tuple-element.56), channel_id=1, source_target_pairs={{0,1},{1,2},{2,3},{3,4},{4,5},{5,6},{6,7},{8,9},{9,10},{10,11},{11... | collective-permute-start | bytes 1179656 | tf_op jit(solution)/shard_map/ppermute | solution.py:14
  537.3 11.8 %collective-permute-start.17 = (f32[256,384]{0,1:T(8,128)S(1)}, f32[256,384]{0,1:T(8,128)S(1)}, u32[]{:S(2)}, u32[]{:S(2)}) collective-permute-start(f32[256,384]{0,1:T(8,128)S(1)} %get-tuple-element.17), channel_id=1, source_target_pairs={{1,0},{2,1},{3,2},{4,3},{5,4},{6,5},{7,6},{9,8},{10,9},{11,10},{12... | collective-permute-start | bytes 1179656 | tf_op jit(solution)/shard_map/ppermute | solution.py:14
  549.5 11.9 %collective-permute-start.16 = (f32[256,384]{0,1:T(8,128)S(1)}, f32[256,384]{0,1:T(8,128)S(1)}, u32[]{:S(2)}, u32[]{:S(2)}) collective-permute-start(f32[256,384]{0,1:T(8,128)S(1)} %get-tuple-element.54), channel_id=1, source_target_pairs={{0,1},{1,2},{2,3},{3,4},{4,5},{5,6},{6,7},{8,9},{9,10},{10,11},{11... | collective-permute-start | bytes 1179656 | tf_op jit(solution)/shard_map/ppermute | solution.py:14
  563.1 10.1 %collective-permute-start.19 = (f32[256,384]{0,1:T(8,128)S(1)}, f32[256,384]{0,1:T(8,128)S(1)}, u32[]{:S(2)}, u32[]{:S(2)}) collective-permute-start(f32[256,384]{0,1:T(8,128)S(1)} %get-tuple-element.11), channel_id=1, source_target_pairs={{1,0},{2,1},{3,2},{4,3},{5,4},{6,5},{7,6},{9,8},{10,9},{11,10},{12... | collective-permute-start | bytes 1179656 | tf_op jit(solution)/shard_map/ppermute | solution.py:14
  574.3 10.9 %collective-permute-start.18 = (f32[256,384]{0,1:T(8,128)}, f32[256,384]{0,1:T(8,128)}, u32[]{:S(2)}, u32[]{:S(2)}) collective-permute-start(f32[256,384]{0,1:T(8,128)} %get-tuple-element.52), channel_id=1, source_target_pairs={{0,1},{1,2},{2,3},{3,4},{4,5},{5,6},{6,7},{8,9},{9,10},{10,11},{11... | collective-permute-start | bytes 1179656 | tf_op jit(solution)/shard_map/ppermute | solution.py:14
  (52 other events, 408.4 us)
Sparse Core Ops, SparseCore 0:
  92.3 35.5 all-reduce.5
  222.9 34.2 all-reduce.7
  352.2 34.2 all-reduce.9
  481.7 34.2 all-reduce.11
where the time goes:
time: 599 us; the launch traced here: 598 us
  waiting for transfers between devices  271 us (45%)
  blocking collectives  179 us (30%)
  starting transfers between devices  55.8 us (9%)
  matrix products  30 us (5%)
  local copies, waits for them, and re-layouts  23.2 us (4%)
  between operations  19.8 us (3%)
  other arithmetic  18.8 us (3%)
    psum x4, waiting for transfers between devices, on_device(): owned = lax.psum(owned, 'group')  138 us
    ppermute x18, waiting for transfers between devices, from_behind(): return lax.ppermute(block, axis, route)  133 us
    all_gather x4, blocking collectives, on_device(): all_terms = lax.all_gather(coarse_terms, 'sub', axis=0, tiled=True)  104 us
    all_to_all x4, blocking collectives, on_device(): lax.all_to_all(partial_vals, 'sub', split_axis=0, concat_axis=0, tiled=True)  59.6 us
    ppermute x18, starting transfers between devices, from_behind(): return lax.ppermute(block, axis, route)  49.6 us
    unnamed x108, local copies, waits for them, and re-layouts  15.7 us
    unnamed x1, blocking collectives  14.9 us
  transfers between devices with their start and end apart: 24, of which 21 were waited for; matrix products, arithmetic and copies ran while one was open for 4% of the time, Pallas kernels for 0%

commit v1 on v0

--- a/solution.py
+++ b/solution.py
@@ -96,7 +96,14 @@
         weighted = (weight * assemble(local, share_up)).astype(jnp.bfloat16)
         coarse_terms = jnp.dot(basis, weighted, preferred_element_type=jnp.float32)
         dof_values = my_dofs.astype(jnp.float32)
-        all_terms = lax.all_gather(coarse_terms, "sub", axis=0, tiled=True)
+        ring = [coarse_terms]
+        for hop in range(7):
+            ring.append(lax.ppermute(ring[-1], "sub", [(dev, (dev + 1) % 8) for dev in range(8)]))
+        all_terms = jnp.roll(
+            jnp.concatenate(ring[::-1], axis=0),
+            (lax.axis_index("sub") + 1) * ring[0].shape[0],
+            axis=0,
+        )
         all_dofs = lax.all_gather(dof_values, "sub", axis=0, tiled=True)
         dof_index = all_dofs.astype(jnp.int32)
         first_row = lax.axis_index("sub") * own_count

time: 599 us -> 656 us (1.095)
  waiting for transfers between devices: 271 us -> 422 us
  blocking collectives: 179 us -> 82.1 us
    ppermute x0 -> x28, waiting for transfers between devices: none -> 131 us  [on_device(): lax.ppermute(ring[-1], 'sub', [(dev, (dev + 1) % 8) for dev in range(8)])]
    all_gather x4 -> x0, blocking collectives: 104 us -> none  [on_device(): all_terms = lax.all_gather(coarse_terms, 'sub', axis=0, tiled=True)]
    psum x4, waiting for transfers between devices: 138 us -> 155 us  [on_device(): owned = lax.psum(owned, 'group')]
    unnamed x1, blocking collectives: 14.9 us -> 22.5 us
    unnamed x108 -> x134, local copies, waits for them, and re-layouts: 15.7 us -> 15.2 us
  transfers between devices with their start and end apart: 24 -> 52, of which waited for: 21 -> 48; matrix products, arithmetic and copies ran while one was open for 4% -> 2% of each run, Pallas kernels for 0% -> 0%
where the time goes in v1:
time: 656 us; the launch traced here: 654 us
  waiting for transfers between devices  422 us (64%)
  blocking collectives  82.1 us (13%)
  starting transfers between devices  60.9 us (9%)
  matrix products  30.1 us (5%)
  local copies, waits for them, and re-layouts  21.8 us (3%)
  between operations  20 us (3%)
  other arithmetic  17.6 us (3%)
    psum x4, waiting for transfers between devices, on_device(): owned = lax.psum(owned, 'group')  155 us
    ppermute x18, waiting for transfers between devices, from_behind(): return lax.ppermute(block, axis, route)  136 us
    ppermute x28, waiting for transfers between devices, on_device(): lax.ppermute(ring[-1], 'sub', [(dev, (dev + 1) % 8) for dev in range(8)])  131 us
    all_to_all x4, blocking collectives, on_device(): lax.all_to_all(partial_vals, 'sub', split_axis=0, concat_axis=0, tiled=True)  59.6 us
    ppermute x18, starting transfers between devices, from_behind(): return lax.ppermute(block, axis, route)  50.1 us
    unnamed x1, blocking collectives  22.5 us
    unnamed x134, local copies, waits for them, and re-layouts  15.2 us
  transfers between devices with their start and end apart: 52, of which 48 were waited for; matrix products, arithmetic and copies ran while one was open for 2% of the time, Pallas kernels for 0%

profile of v1, /device:TPU:16, one launch (start us, length us, event | category | flops | bytes accessed | tf_op | source)
XLA Modules:
  0.0 654.4 jit_solution(1018249831611161389)
XLA Ops:
  61.5 22.5 %all-reduce = f32[256]{0:T(256)S(1)} all-reduce(f32[256]{0:T(256)S(1)} %bitcast_dynamic-update-slice_fusion), channel_id=2, replica_groups=mesh['group'=4,'sub'=8] {'sub'}, use_global_device_ids=true, to_apply=%add | all-reduce | flops 256 | bytes 2048
  101.1 39.0 %all-reduce.6.cloned.1.call-done = f32[64,384]{1,0:T(8,128)} async-done(((f32[64,384]{1,0:T(8,128)}), f32[64,384]{1,0:T(8,128)}) %all-reduce.6.cloned.1.call-update) | async-done | bytes 98320 | tf_op jit(solution)/shard_map/psum | solution.py:114
  141.5 15.0 %all_to_all.20 = f32[8,32,384]{2,1,0:T(8,128)} all-to-all(f32[8,32,384]{2,1,0:T(8,128)S(1)} %bitcast.141), channel_id=1, replica_groups=mesh['group'=4,'sub'=8] {'sub'}, dimensions={0} | all-to-all | bytes 786432 | tf_op jit(solution)/shard_map/all_to_all | solution.py:118
  164.5 8.6 %collective-permute-done.12 = f32[256,384]{0,1:T(8,128)S(1)} collective-permute-done((f32[256,384]{0,1:T(8,128)S(1)}, f32[256,384]{0,1:T(8,128)S(1)}, u32[]{:S(2)}, u32[]{:S(2)}) %collective-permute-start.12) | collective-permute-done | bytes 393248 | tf_op jit(solution)/shard_map/ppermute | solution.py:14
  177.4 7.9 %collective-permute-done.11 = f32[256,384]{0,1:T(8,128)S(1)} collective-permute-done((f32[256,384]{0,1:T(8,128)S(1)}, f32[256,384]{0,1:T(8,128)S(1)}, u32[]{:S(2)}, u32[]{:S(2)}) %collective-permute-start.11) | collective-permute-done | bytes 393248 | tf_op jit(solution)/shard_map/ppermute | solution.py:14
  188.6 8.2 %collective-permute-done.14 = f32[256,384]{0,1:T(8,128)S(1)} collective-permute-done((f32[256,384]{0,1:T(8,128)S(1)}, f32[256,384]{0,1:T(8,128)S(1)}, u32[]{:S(2)}, u32[]{:S(2)}) %collective-permute-start.14) | collective-permute-done | bytes 393248 | tf_op jit(solution)/shard_map/ppermute | solution.py:14
  199.8 8.4 %collective-permute-done.13 = f32[256,384]{0,1:T(8,128)S(1)} collective-permute-done((f32[256,384]{0,1:T(8,128)S(1)}, f32[256,384]{0,1:T(8,128)S(1)}, u32[]{:S(2)}, u32[]{:S(2)}) %collective-permute-start.13) | collective-permute-done | bytes 393248 | tf_op jit(solution)/shard_map/ppermute | solution.py:14
  245.5 38.8 %all-reduce.8.cloned.1.call-done = f32[64,384]{1,0:T(8,128)} async-done(((f32[64,384]{1,0:T(8,128)}), f32[64,384]{1,0:T(8,128)}) %all-reduce.8.cloned.1.call-update) | async-done | bytes 98320 | tf_op jit(solution)/shard_map/psum | solution.py:114
  285.7 14.9 %all_to_all.21 = f32[8,32,384]{2,1,0:T(8,128)} all-to-all(f32[8,32,384]{2,1,0:T(8,128)S(1)} %bitcast.142), channel_id=1, replica_groups=mesh['group'=4,'sub'=8] {'sub'}, dimensions={0} | all-to-all | bytes 786432 | tf_op jit(solution)/shard_map/all_to_all | solution.py:118
  308.7 8.6 %collective-permute-done.23 = f32[256,384]{0,1:T(8,128)S(1)} collective-permute-done((f32[256,384]{0,1:T(8,128)S(1)}, f32[256,384]{0,1:T(8,128)S(1)}, u32[]{:S(2)}, u32[]{:S(2)}) %collective-permute-start.23) | collective-permute-done | bytes 393248 | tf_op jit(solution)/shard_map/ppermute | solution.py:14
  321.8 7.8 %collective-permute-done.22 = f32[256,384]{0,1:T(8,128)S(1)} collective-permute-done((f32[256,384]{0,1:T(8,128)S(1)}, f32[256,384]{0,1:T(8,128)S(1)}, u32[]{:S(2)}, u32[]{:S(2)}) %collective-permute-start.22) | collective-permute-done | bytes 393248 | tf_op jit(solution)/shard_map/ppermute | solution.py:14
  333.0 8.2 %collective-permute-done.25 = f32[256,384]{0,1:T(8,128)S(1)} collective-permute-done((f32[256,384]{0,1:T(8,128)S(1)}, f32[256,384]{0,1:T(8,128)S(1)}, u32[]{:S(2)}, u32[]{:S(2)}) %collective-permute-start.25) | collective-permute-done | bytes 393248 | tf_op jit(solution)/shard_map/ppermute | solution.py:14
  344.1 8.5 %collective-permute-done.24 = f32[256,384]{0,1:T(8,128)S(1)} collective-permute-done((f32[256,384]{0,1:T(8,128)S(1)}, f32[256,384]{0,1:T(8,128)S(1)}, u32[]{:S(2)}, u32[]{:S(2)}) %collective-permute-start.24) | collective-permute-done | bytes 393248 | tf_op jit(solution)/shard_map/ppermute | solution.py:14
  389.9 38.7 %all-reduce.10.cloned.1.call-done = f32[64,384]{1,0:T(8,128)} async-done(((f32[64,384]{1,0:T(8,128)}), f32[64,384]{1,0:T(8,128)}) %all-reduce.10.cloned.1.call-update) | async-done | bytes 98320 | tf_op jit(solution)/shard_map/psum | solution.py:114
  430.0 14.9 %all_to_all.22 = f32[8,32,384]{2,1,0:T(8,128)} all-to-all(f32[8,32,384]{2,1,0:T(8,128)S(1)} %bitcast.143), channel_id=1, replica_groups=mesh['group'=4,'sub'=8] {'sub'}, dimensions={0} | all-to-all | bytes 786432 | tf_op jit(solution)/shard_map/all_to_all | solution.py:118
  453.1 8.6 %collective-permute-done.34 = f32[256,384]{0,1:T(8,128)S(1)} collective-permute-done((f32[256,384]{0,1:T(8,128)S(1)}, f32[256,384]{0,1:T(8,128)S(1)}, u32[]{:S(2)}, u32[]{:S(2)}) %collective-permute-start.34) | collective-permute-done | bytes 393248 | tf_op jit(solution)/shard_map/ppermute | solution.py:14
  466.0 7.9 %collective-permute-done.33 = f32[256,384]{0,1:T(8,128)S(1)} collective-permute-done((f32[256,384]{0,1:T(8,128)S(1)}, f32[256,384]{0,1:T(8,128)S(1)}, u32[]{:S(2)}, u32[]{:S(2)}) %collective-permute-start.33) | collective-permute-done | bytes 393248 | tf_op jit(solution)/shard_map/ppermute | solution.py:14
  477.4 8.2 %collective-permute-done.36 = f32[256,384]{0,1:T(8,128)S(1)} collective-permute-done((f32[256,384]{0,1:T(8,128)S(1)}, f32[256,384]{0,1:T(8,128)S(1)}, u32[]{:S(2)}, u32[]{:S(2)}) %collective-permute-start.36) | collective-permute-done | bytes 393248 | tf_op jit(solution)/shard_map/ppermute | solution.py:14
  488.5 8.5 %collective-permute-done.35 = f32[256,384]{0,1:T(8,128)S(1)} collective-permute-done((f32[256,384]{0,1:T(8,128)S(1)}, f32[256,384]{0,1:T(8,128)S(1)}, u32[]{:S(2)}, u32[]{:S(2)}) %collective-permute-start.35) | collective-permute-done | bytes 393248 | tf_op jit(solution)/shard_map/ppermute | solution.py:14
  534.3 38.7 %all-reduce.12.cloned.1.call-done = f32[64,384]{1,0:T(8,128)} async-done(((f32[64,384]{1,0:T(8,128)}), f32[64,384]{1,0:T(8,128)}) %all-reduce.12.cloned.1.call-update) | async-done | bytes 98320 | tf_op jit(solution)/shard_map/psum | solution.py:114
  574.4 14.9 %all_to_all.23 = f32[8,32,384]{2,1,0:T(8,128)} all-to-all(f32[8,32,384]{2,1,0:T(8,128)S(1)} %bitcast.140), channel_id=1, replica_groups=mesh['group'=4,'sub'=8] {'sub'}, dimensions={0} | all-to-all | bytes 786432 | tf_op jit(solution)/shard_map/all_to_all | solution.py:118
  597.5 8.6 %collective-permute-done.45 = f32[256,384]{0,1:T(8,128)S(1)} collective-permute-done((f32[256,384]{0,1:T(8,128)S(1)}, f32[256,384]{0,1:T(8,128)S(1)}, u32[]{:S(2)}, u32[]{:S(2)}) %collective-permute-start.45) | collective-permute-done | bytes 393248 | tf_op jit(solution)/shard_map/ppermute | solution.py:14
  609.6 8.7 %collective-permute-done.44 = f32[256,384]{0,1:T(8,128)S(1)} collective-permute-done((f32[256,384]{0,1:T(8,128)S(1)}, f32[256,384]{0,1:T(8,128)S(1)}, u32[]{:S(2)}, u32[]{:S(2)}) %collective-permute-start.44) | collective-permute-done | bytes 393248 | tf_op jit(solution)/shard_map/ppermute | solution.py:14
  622.0 8.2 %collective-permute-done.47 = f32[256,384]{0,1:T(8,128)S(1)} collective-permute-done((f32[256,384]{0,1:T(8,128)S(1)}, f32[256,384]{0,1:T(8,128)S(1)}, u32[]{:S(2)}, u32[]{:S(2)}) %collective-permute-start.47) | collective-permute-done | bytes 393248 | tf_op jit(solution)/shard_map/ppermute | solution.py:14
  (305 shorter events, 272.1 us)
Async XLA Ops:
  7.2 132.9 %all-reduce.6.cloned.1.call-start = ((), (), s32[]{:S(2)}) async-start(), calls=%async_computation.4 | async-start | bytes 196608 | tf_op jit(solution)/shard_map/psum | solution.py:114
  14.0 12.7 %collective-permute-start.3 = (f32[256,384]{0,1:T(8,128)S(1)}, f32[256,384]{0,1:T(8,128)S(1)}, u32[]{:S(2)}, u32[]{:S(2)}) collective-permute-start(f32[256,384]{0,1:T(8,128)S(1)} %get-tuple-element.49), channel_id=1, source_target_pairs={{1,0},{2,1},{3,2},{4,3},{5,4},{6,5},{7,6},{9,8},{10,9},{11,10},{12... | collective-permute-start | bytes 1179656 | tf_op jit(solution)/shard_map/ppermute | solution.py:14
  27.8 15.5 %collective-permute-start.2 = (f32[256,384]{0,1:T(8,128)}, f32[256,384]{0,1:T(8,128)}, u32[]{:S(2)}, u32[]{:S(2)}) collective-permute-start(f32[256,384]{0,1:T(8,128)} %get-tuple-element.68), channel_id=1, source_target_pairs={{0,1},{1,2},{2,3},{3,4},{4,5},{5,6},{6,7},{8,9},{9,10},{10,11},{11... | collective-permute-start | bytes 1179656 | tf_op jit(solution)/shard_map/ppermute | solution.py:14
  32.1 9.2 %collective-permute-start.1 = (f32[1,1]{1,0:T(1,128)}, f32[1,1]{1,0:T(1,128)}, u32[]{:S(2)}, u32[]{:S(2)}) collective-permute-start(f32[1,1]{1,0:T(1,128)} %param.13), channel_id=1, source_target_pairs={{1,0},{2,1},{3,2},{4,3},{5,4},{6,5},{7,6},{9,8},{10,9},{11,10},{12... | collective-permute-start | bytes 20 | tf_op jit(solution)/shard_map/ppermute | solution.py:25
  61.4 22.6 %collective-permute-start.7 = (f32[32,384]{1,0:T(8,128)S(1)}, f32[32,384]{1,0:T(8,128)S(1)}, u32[]{:S(2)}, u32[]{:S(2)}) collective-permute-start(f32[32,384]{1,0:T(8,128)S(1)} %collective-permute-done.6), channel_id=1, source_target_pairs={{0,1},{1,2},{2,3},{3,4},{4,5},{5,6},{6,7},{7,0},{8,9},{9,10},{10,1... | collective-permute-start | bytes 147464 | tf_op jit(solution)/shard_map/ppermute | solution.py:101
  100.2 184.1 %all-reduce.8.cloned.1.call-start = ((), (), s32[]{:S(2)}) async-start(), calls=%async_computation.5 | async-start | bytes 196608 | tf_op jit(solution)/shard_map/psum | solution.py:114
  161.3 11.8 %collective-permute-start.12 = (f32[256,384]{0,1:T(8,128)S(1)}, f32[256,384]{0,1:T(8,128)S(1)}, u32[]{:S(2)}, u32[]{:S(2)}) collective-permute-start(f32[256,384]{0,1:T(8,128)S(1)} %get-tuple-element.45), channel_id=1, source_target_pairs={{1,0},{2,1},{3,2},{4,3},{5,4},{6,5},{7,6},{9,8},{10,9},{11,10},{12... | collective-permute-start | bytes 1179656 | tf_op jit(solution)/shard_map/ppermute | solution.py:14
  173.4 11.9 %collective-permute-start.11 = (f32[256,384]{0,1:T(8,128)S(1)}, f32[256,384]{0,1:T(8,128)S(1)}, u32[]{:S(2)}, u32[]{:S(2)}) collective-permute-start(f32[256,384]{0,1:T(8,128)S(1)} %get-tuple-element.64), channel_id=1, source_target_pairs={{0,1},{1,2},{2,3},{3,4},{4,5},{5,6},{6,7},{8,9},{9,10},{10,11},{11... | collective-permute-start | bytes 1179656 | tf_op jit(solution)/shard_map/ppermute | solution.py:14
  186.7 10.1 %collective-permute-start.14 = (f32[256,384]{0,1:T(8,128)S(1)}, f32[256,384]{0,1:T(8,128)S(1)}, u32[]{:S(2)}, u32[]{:S(2)}) collective-permute-start(f32[256,384]{0,1:T(8,128)S(1)} %get-tuple-element.39), channel_id=1, source_target_pairs={{1,0},{2,1},{3,2},{4,3},{5,4},{6,5},{7,6},{9,8},{10,9},{11,10},{12... | collective-permute-start | bytes 1179656 | tf_op jit(solution)/shard_map/ppermute | solution.py:14
  197.1 11.1 %collective-permute-start.13 = (f32[256,384]{0,1:T(8,128)S(1)}, f32[256,384]{0,1:T(8,128)S(1)}, u32[]{:S(2)}, u32[]{:S(2)}) collective-permute-start(f32[256,384]{0,1:T(8,128)S(1)} %get-tuple-element.62), channel_id=1, source_target_pairs={{0,1},{1,2},{2,3},{3,4},{4,5},{5,6},{6,7},{8,9},{9,10},{10,11},{11... | collective-permute-start | bytes 1179656 | tf_op jit(solution)/shard_map/ppermute | solution.py:14
  245.4 183.2 %all-reduce.10.cloned.1.call-start = ((), (), s32[]{:S(2)}) async-start(), calls=%async_computation.6 | async-start | bytes 196608 | tf_op jit(solution)/shard_map/psum | solution.py:114
  305.5 11.8 %collective-permute-start.23 = (f32[256,384]{0,1:T(8,128)S(1)}, f32[256,384]{0,1:T(8,128)S(1)}, u32[]{:S(2)}, u32[]{:S(2)}) collective-permute-start(f32[256,384]{0,1:T(8,128)S(1)} %get-tuple-element.35), channel_id=1, source_target_pairs={{1,0},{2,1},{3,2},{4,3},{5,4},{6,5},{7,6},{9,8},{10,9},{11,10},{12... | collective-permute-start | bytes 1179656 | tf_op jit(solution)/shard_map/ppermute | solution.py:14
  317.7 11.9 %collective-permute-start.22 = (f32[256,384]{0,1:T(8,128)S(1)}, f32[256,384]{0,1:T(8,128)S(1)}, u32[]{:S(2)}, u32[]{:S(2)}) collective-permute-start(f32[256,384]{0,1:T(8,128)S(1)} %get-tuple-element.60), channel_id=1, source_target_pairs={{0,1},{1,2},{2,3},{3,4},{4,5},{5,6},{6,7},{8,9},{9,10},{10,11},{11... | collective-permute-start | bytes 1179656 | tf_op jit(solution)/shard_map/ppermute | solution.py:14
  331.0 10.1 %collective-permute-start.25 = (f32[256,384]{0,1:T(8,128)S(1)}, f32[256,384]{0,1:T(8,128)S(1)}, u32[]{:S(2)}, u32[]{:S(2)}) collective-permute-start(f32[256,384]{0,1:T(8,128)S(1)} %get-tuple-element.29), channel_id=1, source_target_pairs={{1,0},{2,1},{3,2},{4,3},{5,4},{6,5},{7,6},{9,8},{10,9},{11,10},{12... | collective-permute-start | bytes 1179656 | tf_op jit(solution)/shard_map/ppermute | solution.py:14
  341.5 11.1 %collective-permute-start.24 = (f32[256,384]{0,1:T(8,128)S(1)}, f32[256,384]{0,1:T(8,128)S(1)}, u32[]{:S(2)}, u32[]{:S(2)}) collective-permute-start(f32[256,384]{0,1:T(8,128)S(1)} %get-tuple-element.58), channel_id=1, source_target_pairs={{0,1},{1,2},{2,3},{3,4},{4,5},{5,6},{6,7},{8,9},{9,10},{10,11},{11... | collective-permute-start | bytes 1179656 | tf_op jit(solution)/shard_map/ppermute | solution.py:14
  389.8 183.2 %all-reduce.12.cloned.1.call-start = ((), (), s32[]{:S(2)}) async-start(), calls=%async_computation.7 | async-start | bytes 196608 | tf_op jit(solution)/shard_map/psum | solution.py:114
  449.9 11.8 %collective-permute-start.34 = (f32[256,384]{0,1:T(8,128)S(1)}, f32[256,384]{0,1:T(8,128)S(1)}, u32[]{:S(2)}, u32[]{:S(2)}) collective-permute-start(f32[256,384]{0,1:T(8,128)S(1)} %get-tuple-element.25), channel_id=1, source_target_pairs={{1,0},{2,1},{3,2},{4,3},{5,4},{6,5},{7,6},{9,8},{10,9},{11,10},{12... | collective-permute-start | bytes 1179656 | tf_op jit(solution)/shard_map/ppermute | solution.py:14
  462.0 11.9 %collective-permute-start.33 = (f32[256,384]{0,1:T(8,128)S(1)}, f32[256,384]{0,1:T(8,128)S(1)}, u32[]{:S(2)}, u32[]{:S(2)}) collective-permute-start(f32[256,384]{0,1:T(8,128)S(1)} %get-tuple-element.56), channel_id=1, source_target_pairs={{0,1},{1,2},{2,3},{3,4},{4,5},{5,6},{6,7},{8,9},{9,10},{10,11},{11... | collective-permute-start | bytes 1179656 | tf_op jit(solution)/shard_map/ppermute | solution.py:14
  475.5 10.1 %collective-permute-start.36 = (f32[256,384]{0,1:T(8,128)S(1)}, f32[256,384]{0,1:T(8,128)S(1)}, u32[]{:S(2)}, u32[]{:S(2)}) collective-permute-start(f32[256,384]{0,1:T(8,128)S(1)} %get-tuple-element.19), channel_id=1, source_target_pairs={{1,0},{2,1},{3,2},{4,3},{5,4},{6,5},{7,6},{9,8},{10,9},{11,10},{12... | collective-permute-start | bytes 1179656 | tf_op jit(solution)/shard_map/ppermute | solution.py:14
  485.9 11.1 %collective-permute-start.35 = (f32[256,384]{0,1:T(8,128)S(1)}, f32[256,384]{0,1:T(8,128)S(1)}, u32[]{:S(2)}, u32[]{:S(2)}) collective-permute-start(f32[256,384]{0,1:T(8,128)S(1)} %get-tuple-element.54), channel_id=1, source_target_pairs={{0,1},{1,2},{2,3},{3,4},{4,5},{5,6},{6,7},{8,9},{9,10},{10,11},{11... | collective-permute-start | bytes 1179656 | tf_op jit(solution)/shard_map/ppermute | solution.py:14
  594.3 11.8 %collective-permute-start.45 = (f32[256,384]{0,1:T(8,128)S(1)}, f32[256,384]{0,1:T(8,128)S(1)}, u32[]{:S(2)}, u32[]{:S(2)}) collective-permute-start(f32[256,384]{0,1:T(8,128)S(1)} %get-tuple-element.15), channel_id=1, source_target_pairs={{1,0},{2,1},{3,2},{4,3},{5,4},{6,5},{7,6},{9,8},{10,9},{11,10},{12... | collective-permute-start | bytes 1179656 | tf_op jit(solution)/shard_map/ppermute | solution.py:14
  606.4 11.9 %collective-permute-start.44 = (f32[256,384]{0,1:T(8,128)S(1)}, f32[256,384]{0,1:T(8,128)S(1)}, u32[]{:S(2)}, u32[]{:S(2)}) collective-permute-start(f32[256,384]{0,1:T(8,128)S(1)} %get-tuple-element.52), channel_id=1, source_target_pairs={{0,1},{1,2},{2,3},{3,4},{4,5},{5,6},{6,7},{8,9},{9,10},{10,11},{11... | collective-permute-start | bytes 1179656 | tf_op jit(solution)/shard_map/ppermute | solution.py:14
  620.0 10.1 %collective-permute-start.47 = (f32[256,384]{0,1:T(8,128)S(1)}, f32[256,384]{0,1:T(8,128)S(1)}, u32[]{:S(2)}, u32[]{:S(2)}) collective-permute-start(f32[256,384]{0,1:T(8,128)S(1)} %get-tuple-element.9), channel_id=1, source_target_pairs={{1,0},{2,1},{3,2},{4,3},{5,4},{6,5},{7,6},{9,8},{10,9},{11,10},{12... | collective-permute-start | bytes 1179656 | tf_op jit(solution)/shard_map/ppermute | solution.py:14
  631.2 10.9 %collective-permute-start.46 = (f32[256,384]{0,1:T(8,128)}, f32[256,384]{0,1:T(8,128)}, u32[]{:S(2)}, u32[]{:S(2)}) collective-permute-start(f32[256,384]{0,1:T(8,128)} %get-tuple-element.50), channel_id=1, source_target_pairs={{0,1},{1,2},{2,3},{3,4},{4,5},{5,6},{6,7},{8,9},{9,10},{10,11},{11... | collective-permute-start | bytes 1179656 | tf_op jit(solution)/shard_map/ppermute | solution.py:14
  (79 other events, 608.7 us)
Sparse Core Ops, SparseCore 0:
  100.3 39.7 all-reduce.5
  245.6 38.6 all-reduce.7
  389.9 38.6 all-reduce.9
  534.4 38.5 all-reduce.11
